TPU v7x, 512 devices: a 8x2x16 block of a 8x16x16 slice. The times are simulated.
512 devices in a mesh: groups: 2 (over y), seq: 32 (over z, core), rep: 8 (over x).
Axes of the slice: x: 8, y: 2, z: 16, core: 2. Of those that a mesh axis runs over, the one named last changes fastest.
The devices are a block of a 8x16x16 slice.
Arguments:
- queries: bfloat16 [1024, 4096], P(('groups', 'seq'), 'rep'), parts along dimension 0, may hold values from -128 to 128
- keys_new: bfloat16 [1024, 1024], P(('groups', 'seq'), 'rep'), parts along dimension 0, may hold values from -4 to 4
- values_new: bfloat16 [1024, 1024], P(('groups', 'seq'), 'rep'), parts along dimension 0, may hold values from -6 to 6
- keys_past: bfloat16 [16384, 1024], P(('groups', 'seq'), 'rep'), parts along dimension 0, may hold values from -4 to 4
- values_past: bfloat16 [16384, 1024], P(('groups', 'seq'), 'rep'), parts along dimension 0, may hold values from -6 to 6
- block_order: int32 [64], P('groups'), parts along dimension 0, may hold values from 0 to 31, each once
- residual: bfloat16 [1024, 4096], P(('groups', 'seq'), 'rep'), parts along dimension 0, may hold values from -6 to 6
- out_proj: bfloat16 [4096, 4096], P('seq', 'rep'), may hold values from -0.09375 to 0.09375
- norm_gain: float32 [4096], replicated, may hold values from 0.5 to 1.5
- router: float32 [4096, 4], replicated, may hold values from -0.09375 to 0.09375
- w_gate: bfloat16 [8, 4096, 4096], P('rep', None, 'seq'), may hold values from -0.09375 to 0.09375
- w_up: bfloat16 [8, 4096, 4096], P('rep', None, 'seq'), may hold values from -0.09375 to 0.09375
- w_down: bfloat16 [8, 4096, 4096], P('rep', 'seq'), may hold values from -0.0625 to 0.0625
- expert_ids: int32 [1024, 2], P(('groups', 'seq')), parts along dimension 0, may hold values from 0 to 3, all different within a row; in each aligned block of 16 rows (0 to 15, 16 to 31, ...) at most 12 rows name the same one
Outputs:
- attended: bfloat16 [1024, 4096], P(('groups', 'seq'), 'rep'), parts along dimension 0
- layer_out: bfloat16 [1024, 4096], P(('groups', 'seq'), 'rep'), parts along dimension 0
- keys_cache: bfloat16 [1024, 1024], P(('groups', 'seq')), parts along dimension 0
- values_cache: bfloat16 [1024, 1024], P(('groups', 'seq')), parts along dimension 0
There are 2 independent parts, one for each index of `groups`. A program takes and returns all parts, laid end to end along the dimension named above; an argument that names none is the same for every part. Nothing has to cross between parts.
Inputs may be any that keep to these rules, and one draw needn't show every extreme that they name: `block_order`: each block index 0 to 32 - 1 appears once. `expert_ids`: each row names 2 different experts; in the rows of one device (aligned blocks of 16 rows) no expert is named by more than 12 rows, and in some block one expert is named by exactly 12.
All inputs are finite; a program needn't handle non-finite values.
Results may differ from a plain program's by a relative error of at most 0.011.
Values may be sent and summed in bfloat16 or wider, within the bound.
A program may use at most 64 MiB of HBM per device.

v0:
```python
import math
import jax
import jax.numpy as jnp
from jax import lax
from jax.sharding import Mesh
from jax.sharding import PartitionSpec as P

EXPERTS = 4
CAP = 12
SEQ = ("seq_0", "seq_1")
GROUPS_SEQ = ("groups", "seq_0", "seq_1")


def in_one_piece(arrays, axis, dim, along):
    both = jnp.concatenate(arrays, axis=along)
    out, at, gathered = (lax.all_gather(both, axis, axis=dim, tiled=True), 0, [])
    for a in arrays:
        gathered.append(lax.slice_in_dim(out, at, at + a.shape[along], axis=along))
        at += a.shape[along]
    return tuple(gathered)


def sent_to_all(array, axis):
    size = lax.axis_size(axis)
    return lax.all_to_all(
        jnp.broadcast_to(array[None], (size, *array.shape)), axis, 0, 0, tiled=True
    )


def laid_out(tiles, dim):
    tiles = jnp.moveaxis(tiles, 0, dim)
    shape = tiles.shape
    return tiles.reshape(*shape[:dim], shape[dim] * shape[dim + 1], *shape[dim + 2 :])


def gather_directly(array, axis, dim):
    tiles = sent_to_all(array, axis)
    return laid_out(tiles, dim)


def own_block(tiles, axes, order):
    shape = [lax.axis_size(a) for a in axes]
    tiles = tiles.reshape(*shape, *tiles.shape[1:])
    tiles = tiles.transpose(*order, *range(len(axes), tiles.ndim))
    tiles = tiles.reshape(-1, *tiles.shape[len(axes) :])
    for k in order:
        tiles = lax.psum_scatter(tiles, axes[k], scatter_dimension=0, tiled=True)
    return tiles[0]


def in_blocks(array, dim, size):
    shape = array.shape
    tiles = array.reshape(*shape[:dim], size, shape[dim] // size, *shape[dim + 1 :])
    return jnp.moveaxis(tiles, dim, 0)


def sum_by_axis(array, axes, order, dim):
    size = lax.axis_size(axes)
    return own_block(in_blocks(array, dim, size), axes, order)


def block_lookup(owners, block_order):
    width = block_order.shape[0]
    hits = owners[:, None] == jnp.arange(width, dtype=jnp.int32)[None, :]
    return jnp.sum(jnp.where(hits, block_order[None, :], 0), axis=1)


def body(
    queries,
    keys_new,
    values_new,
    keys_past,
    values_past,
    block_order,
    residual,
    out_proj,
    norm_gain,
    router,
    w_gate,
    w_up,
    w_down,
    expert_ids,
):
    seq_index = lax.axis_index(SEQ)
    rep_index = lax.axis_index("rep")
    rep_count = lax.axis_size("rep")
    tok_count = queries.shape[0]
    head_dim = keys_new.shape[1]
    q_per = queries.shape[1] // head_dim
    past_len = keys_past.shape[0]
    key_span = past_len + tok_count
    row_total = tok_count * q_per
    my_block = block_lookup(jnp.full((1,), seq_index, jnp.int32), block_order)[0]
    scaling = 1.0 / math.sqrt(head_dim)
    query_rows = queries.reshape(row_total, head_dim)
    query_pos = my_block * tok_count + jnp.arange(row_total, dtype=jnp.int32) // q_per
    keys_local = jnp.concatenate([keys_past, keys_new], axis=0)
    values_local = jnp.concatenate([values_past, values_new], axis=0)
    running = jnp.full((row_total,), -1e30, jnp.float32)
    key_piece, value_piece = in_one_piece((keys_local, values_local), SEQ, 0, 1)
    row_count = key_piece.shape[0]
    key_index = jnp.arange(row_count, dtype=jnp.int32)
    key_owner = key_index // key_span
    offset = key_index % key_span
    key_pos = block_lookup(key_owner, block_order) * tok_count + offset - past_len
    visible = (offset < past_len)[None, :] | (key_pos[None, :] <= query_pos[:, None])
    scores = jnp.dot(query_rows, key_piece.T, preferred_element_type=jnp.float32) * scaling
    highest = jnp.maximum(running, jnp.max(jnp.where(visible, scores, -1e30), axis=1))
    weights = jnp.where(visible, jnp.exp(scores - highest[:, None]), 0.0)
    totals = jnp.sum(weights, axis=1)
    numerator = jnp.dot(
        weights.astype(jnp.bfloat16), value_piece, preferred_element_type=jnp.float32
    )
    running, totals, numerator = (highest, totals, numerator)
    attn_local = (
        (numerator / totals[:, None]).reshape(tok_count, q_per * head_dim).astype(jnp.bfloat16)
    )
    attn_full, keys_cache, values_cache = (
        lax.all_gather(attn_local, "rep", axis=1, tiled=True),
        *in_one_piece((keys_new, values_new), "rep", 1, 0),
    )
    projected = jnp.dot(
        attn_full,
        lax.all_gather(out_proj, SEQ, axis=0, tiled=True),
        preferred_element_type=jnp.float32,
    )
    attended = (residual.astype(jnp.float32) + projected).astype(jnp.bfloat16)
    full_rows = gather_directly(attended, "rep", 1)
    features = full_rows.astype(jnp.float32)
    mean_square = jnp.mean(features * features, axis=1, keepdims=True)
    normed = (features * norm_gain[None, :] * lax.rsqrt(mean_square + 1e-05)).astype(jnp.bfloat16)
    logits = jnp.dot(normed.astype(jnp.float32), router, precision=lax.Precision.HIGHEST)
    expert_range = jnp.arange(EXPERTS, dtype=jnp.int32)
    first_pick = (expert_ids[:, 0:1] == expert_range[None, :]).astype(jnp.float32)
    second_pick = (expert_ids[:, 1:2] == expert_range[None, :]).astype(jnp.float32)
    share_first = jax.nn.sigmoid(
        jnp.sum(first_pick * logits, axis=1) - jnp.sum(second_pick * logits, axis=1)
    )
    token_share = share_first[:, None] * first_pick + (1.0 - share_first)[:, None] * second_pick
    member = first_pick + second_pick
    ranking = jnp.cumsum(member, axis=0) - member
    slot_range = jnp.arange(CAP, dtype=jnp.float32)
    selection = member.T[:, None, :] * (ranking.T[:, None, :] == slot_range[None, :, None]).astype(
        jnp.float32
    )
    mine_mask = (expert_range == rep_index % EXPERTS).astype(jnp.float32)
    my_selection = jnp.einsum("e,ejt->jt", mine_mask, selection)
    slot_rows = jnp.dot(
        my_selection.astype(jnp.bfloat16), normed, preferred_element_type=jnp.float32
    ).astype(jnp.bfloat16)
    gate_local = w_gate[0]
    up_local = w_up[0]
    down_local = w_down[0]
    piece = lax.all_gather(slot_rows, SEQ, axis=0, tiled=True)
    gate_part = jnp.dot(piece, gate_local, preferred_element_type=jnp.float32)
    up_part = jnp.dot(piece, up_local, preferred_element_type=jnp.float32)
    hidden_slots = (jax.nn.silu(gate_part) * up_part).astype(jnp.bfloat16)
    expert_part = sum_by_axis(
        jnp.dot(hidden_slots, down_local, preferred_element_type=jnp.float32).astype(jnp.bfloat16),
        SEQ,
        (1, 0),
        0,
    ).astype(jnp.float32)
    returned = lax.all_to_all(
        expert_part.astype(jnp.bfloat16), "rep", split_axis=1, concat_axis=0, tiled=True
    ).astype(expert_part.dtype)
    source_expert = jnp.arange(rep_count, dtype=jnp.int32) % EXPERTS
    source_pick = (source_expert[:, None] == expert_range[None, :]).astype(jnp.float32)
    combine = jnp.einsum("re,ejt,te->trj", source_pick, selection, token_share).reshape(
        tok_count, rep_count * CAP
    )
    moe_slice = jnp.dot(combine, returned, precision=lax.Precision.HIGHEST)
    layer_out = (attended.astype(jnp.float32) + moe_slice).astype(jnp.bfloat16)
    return (attended, layer_out, keys_cache, values_cache)


def solution(mesh):
    split = Mesh(
        mesh.devices.reshape(mesh.shape["groups"], 16, 2, mesh.shape["rep"]),
        ("groups", "seq_0", "seq_1", "rep"),
    )
    return jax.shard_map(
        body,
        mesh=split,
        in_specs=(
            P(GROUPS_SEQ, "rep"),
            P(GROUPS_SEQ, "rep"),
            P(GROUPS_SEQ, "rep"),
            P(GROUPS_SEQ, "rep"),
            P(GROUPS_SEQ, "rep"),
            P("groups"),
            P(GROUPS_SEQ, "rep"),
            P(SEQ, "rep"),
            P(),
            P(),
            P("rep", None, SEQ),
            P("rep", None, SEQ),
            P("rep", SEQ, None),
            P(GROUPS_SEQ, None),
        ),
        out_specs=(
            P(GROUPS_SEQ, "rep"),
            P(GROUPS_SEQ, "rep"),
            P(GROUPS_SEQ, None),
            P(GROUPS_SEQ, None),
        ),
        check_vma=False,
    )
```

profile of v0, /device:TPU:66, one launch (start us, length us, event | category | flops | bytes accessed | tf_op | source)
XLA Modules:
  0.0 435.2 jit_solution(9324647808169427397)
XLA Ops:
  7.2 0.0 copy-start
  7.2 0.1 all-gather.5.cloned.1.call-start
  7.3 1.7 maximum_maximum_fusion
  8.9 0.1 all-gather.5.cloned.1.call-update
  9.0 0.1 all-gather.7.cloned.1.call-start
  9.0 0.7 all-gather.7.cloned.1.call-update
  9.8 0.7 reshape.156
  10.5 1.3 fusion.64
  12.5 0.9 select_reduce_fusion.1
  13.5 106.4 %all-gather.5.cloned.1.call-done = bf16[8704,256]{1,0:T(8,128)(2,1)} async-done(((bf16[272,256]{1,0:T(8,128)(2,1)}), bf16[8704,256]{1,0:T(8,128)(2,1)}) %all-gather.5.cloned.1.call-update) | async-done | bytes 4456464 | tf_op jit(solution)/shard_map/all_gather | solution.py:16
  119.9 0.0 copy-start.10
  119.9 2.8 select_reduce_fusion
  122.7 0.9 fusion.5
  123.6 0.0 copy-done.10
  123.6 0.0 copy-start.6
  123.6 0.8 fusion.22
  124.5 24.7 %all_gather.16 = bf16[16,4096]{1,0:T(8,128)(2,1)S(1)} all-gather(bf16[16,512]{1,0:T(8,128)(2,1)S(1)} %convert_element_type.81), channel_id=1, replica_groups=mesh['groups'=2,'seq_0'=16,'seq_1'=2,'rep'=8] {'rep'}, dimensions={1}, use_global_device_ids=true | all-gather | bytes 147456 | tf_op jit(solution)/shard_map/all_gather | solution.py:119
  149.2 44.8 %all-gather.7.cloned.1.call-done = bf16[4096,512]{1,0:T(8,128)(2,1)} async-done(((bf16[128,512]{1,0:T(8,128)(2,1)}), bf16[4096,512]{1,0:T(8,128)(2,1)}) %all-gather.7.cloned.1.call-update) | async-done | bytes 4194320 | tf_op jit(solution)/shard_map/all_gather | solution.py:124
  194.0 0.0 copy-done.6
  194.0 2.8 fusion.16
  196.8 0.7 broadcast_in_dim.33
  197.5 7.2 %all-to-all-start = ((bf16[8,16,512]{2,1,0:T(8,128)(2,1)}), bf16[8,16,512]{2,1,0:T(8,128)(2,1)S(1)}, u32[]{:S(2)}, u32[]{:S(2)}) async-start(bf16[8,16,512]{2,1,0:T(8,128)(2,1)} %broadcast_in_dim.33), calls=%async_computation | async-start | bytes 262144 | tf_op jit(solution)/shard_map/all_to_all | solution.py:25
  204.7 0.0 all-gather.9.cloned.1.call-start
  204.7 0.0 copy-done.9
  204.8 8.0 %all-to-all-done = bf16[8,16,512]{2,1,0:T(8,128)(2,1)S(1)} async-done(((bf16[8,16,512]{2,1,0:T(8,128)(2,1)}), bf16[8,16,512]{2,1,0:T(8,128)(2,1)S(1)}, u32[]{:S(2)}, u32[]{:S(2)}) %all-to-all-start) | async-done | bytes 131104 | tf_op jit(solution)/shard_map/all_to_all | solution.py:25
  212.8 0.1 fusion.32
  212.9 0.0 copy-done.4
  213.0 0.0 copy-done.5
  213.0 0.3 select_reduce_fusion.2
  213.3 0.1 copy.48
  213.5 0.1 copy.49
  213.5 0.1 fusion.47
  213.7 0.9 fusion.1
  214.6 0.1 all-gather.9.cloned.1.call-update
  214.6 0.0 copy-start.1
  214.6 0.1 reduce-scatter.3.cloned.1.call-start
  214.7 68.2 %all-gather.9.cloned.1.call-done = bf16[32,12,4096]{2,1,0:T(8,128)(2,1)} async-done(((bf16[1,12,4096]{2,1,0:T(8,128)(2,1)}), bf16[32,12,4096]{2,1,0:T(8,128)(2,1)}) %all-gather.9.cloned.1.call-update) | async-done | bytes 3145744 | tf_op jit(solution)/shard_map/all_gather | solution.py:154
  282.9 5.6 %reshape.160 = bf16[384,4096]{1,0:T(8,128)(2,1)} reshape(bf16[32,12,4096]{2,1,0:T(8,128)(2,1)} %all-gather.9.cloned.1.call-done) | data formatting | bytes 6291456
  288.5 0.0 copy-done.1
  288.5 2.9 fusion.30
  291.5 0.0 copy-done
  291.5 0.0 copy-done.2
  291.5 7.0 %convolution_convert_fusion = bf16[384,4096]{1,0:T(8,128)(2,1)} fusion(bf16[384,4096]{1,0:T(8,128)(2,1)} %reshape.160, bf16[1,128,4096]{2,1,0:T(8,128)(2,1)S(1)} %copy-done, bf16[1,4096,128]{2,1,0:T(8,128)(2,1)S(1)} %copy-done.2, f32[384,128]{1,0:T(8,128)S(1)} %fusion.30), kind=kOutput, calls=%fused_computation.2 | convolution fusion | flops 807174144 | bytes 8585216 | tf_op jit(solution)/shard_map/dot_general | solution.py:159
  298.5 5.5 %reshape_reshape.3 = bf16[16,2,12,4096]{3,2,1,0:T(8,128)(2,1)} reshape(bf16[384,4096]{1,0:T(8,128)(2,1)} %convolution_convert_fusion) | data formatting | bytes 6291456 | tf_op jit(solution)/shard_map/reshape;reshape | solution.py:43
  304.0 5.6 %copy.51 = bf16[2,16,12,4096]{3,1,0,2:T(8,128)(2,1)} copy(bf16[2,16,12,4096]{3,2,0,1:T(8,128)(2,1)} %bitcast.62) | data formatting | bytes 6291456 | tf_op jit(solution)/shard_map/transpose | solution.py:44
  309.6 0.1 reduce-scatter.3.cloned.1.call-update
  309.7 0.0 copy-start.7
  309.7 0.0 copy-start.8
  309.7 0.2 reduce-scatter.5.cloned.1.call-start
  309.9 19.5 %reduce-scatter.3.cloned.1.call-done = bf16[16,12,4096]{2,0,1:T(8,128)(2,1)} async-done(((bf16[32,12,4096]{2,0,1:T(8,128)(2,1)}), bf16[16,12,4096]{2,0,1:T(8,128)(2,1)}) %reduce-scatter.3.cloned.1.call-update) | async-done | bytes 1572880 | tf_op jit(solution)/shard_map/reduce_scatter | solution.py:47
  329.5 3.7 copy.52
  333.1 0.1 reduce-scatter.5.cloned.1.call-update
  333.2 0.0 copy-done.7
  333.2 0.0 copy-done.8
  333.2 22.3 %all_gather.19 = bf16[32,1024]{1,0:T(8,128)(2,1)S(1)} all-gather(bf16[32,128]{1,0:T(8,128)(2,1)S(1)} %pad_maximum_fusion), channel_id=1, replica_groups=mesh['groups'=2,'seq_0'=16,'seq_1'=2,'rep'=8] {'rep'}, dimensions={1}, use_global_device_ids=true | all-gather | bytes 73728 | tf_op jit(solution)/shard_map/all_gather | solution.py:16
  355.6 0.6 fusion.72
  356.2 54.9 %reduce-scatter.5.cloned.1.call-done = bf16[1,12,4096]{2,1,0:T(8,128)(2,1)} async-done(((bf16[16,12,4096]{2,1,0:T(8,128)(2,1)}), bf16[1,12,4096]{2,1,0:T(8,128)(2,1)}) %reduce-scatter.5.cloned.1.call-update) | async-done | bytes 98320 | tf_op jit(solution)/shard_map/reduce_scatter | solution.py:47
  411.1 0.9 copy.57
  412.0 0.7 copy.53
  412.7 7.4 %all-to-all-start.1 = ((bf16[12,8,512]{2,0,1:T(8,128)(2,1)}), bf16[12,8,512]{2,0,1:T(8,128)(2,1)S(1)}, u32[]{:S(2)}, u32[]{:S(2)}) async-start(bf16[12,8,512]{2,0,1:T(8,128)(2,1)} %copy.53), calls=%async_computation.3 | async-start | bytes 262144 | tf_op jit(solution)/shard_map/all_to_all | solution.py:164
  420.2 0.2 convolution_bitcast_fusion
  420.4 7.4 %all-to-all-done.1 = bf16[12,8,512]{2,0,1:T(8,128)(2,1)S(1)} async-done(((bf16[12,8,512]{2,0,1:T(8,128)(2,1)}), bf16[12,8,512]{2,0,1:T(8,128)(2,1)S(1)}, u32[]{:S(2)}, u32[]{:S(2)}) %all-to-all-start.1) | async-done | bytes 98336 | tf_op jit(solution)/shard_map/all_to_all | solution.py:164
  427.8 0.0 copy-done.3
  427.8 0.8 fusion.15
  (22 shorter events, 0.2 us)
Async XLA Ops:
  7.2 284.3 %copy-start = (bf16[1,128,4096]{2,1,0:T(8,128)(2,1)S(1)}, bf16[1,128,4096]{2,1,0:T(8,128)(2,1)}, u32[]{:S(2)}) copy-start(bf16[1,128,4096]{2,1,0:T(8,128)(2,1)} %param.26) | copy-start | bytes 3145732
  7.2 112.7 %all-gather.5.cloned.1.call-start = ((), (), s32[]{:S(2)}) async-start(), calls=%async_computation.4 | async-start | bytes 4595712 | tf_op jit(solution)/shard_map/all_gather | solution.py:16
  9.0 185.0 %all-gather.7.cloned.1.call-start = ((), (), s32[]{:S(2)}) async-start(), calls=%async_computation.5 | async-start | bytes 4325376 | tf_op jit(solution)/shard_map/all_gather | solution.py:124
  119.9 3.7 copy-start.10
  123.6 70.4 %copy-start.6 = (bf16[16,512]{1,0:T(8,128)(2,1)S(1)}, bf16[16,512]{1,0:T(8,128)(2,1)}, u32[]{:S(2)}) copy-start(bf16[16,512]{1,0:T(8,128)(2,1)} %param.20) | copy-start | bytes 49156
  149.2 55.5 %copy-start.9 = (s32[16,2]{0,1:T(2,128)S(1)}, s32[16,2]{0,1:T(2,128)}, u32[]{:S(2)}) copy-start(s32[16,2]{0,1:T(2,128)} %param.27) | copy-start | bytes 388
  149.2 63.7 %copy-start.4 = (f32[4096,4]{0,1:T(4,128)S(1)}, f32[4096,4]{0,1:T(4,128)}, u32[]{:S(2)}) copy-start(f32[4096,4]{0,1:T(4,128)} %param.23) | copy-start | bytes 196612
  149.2 63.8 %copy-start.5 = (f32[4096]{0:T(1024)S(1)}, f32[4096]{0:T(1024)}, u32[]{:S(2)}) copy-start(f32[4096]{0:T(1024)} %param.22) | copy-start | bytes 49156
  196.8 231.0 %copy-start.3 = (bf16[16,512]{1,0:T(8,128)(2,1)}, bf16[16,512]{1,0:T(8,128)(2,1)S(1)}, u32[]{:S(2)}) copy-start(bf16[16,512]{1,0:T(8,128)(2,1)S(1)} %fusion.16) | copy-start | bytes 49156
  197.5 15.2 %all-to-all-start = ((bf16[8,16,512]{2,1,0:T(8,128)(2,1)}), bf16[8,16,512]{2,1,0:T(8,128)(2,1)S(1)}, u32[]{:S(2)}, u32[]{:S(2)}) async-start(bf16[8,16,512]{2,1,0:T(8,128)(2,1)} %broadcast_in_dim.33), calls=%async_computation | async-start | bytes 262144 | tf_op jit(solution)/shard_map/all_to_all | solution.py:25
  204.7 78.2 %all-gather.9.cloned.1.call-start = ((), (), s32[]{:S(2)}) async-start(), calls=%async_computation.8 | async-start | bytes 4325376 | tf_op jit(solution)/shard_map/all_gather | solution.py:154
  214.6 73.9 %copy-start.1 = (bf16[1,4096,128]{2,1,0:T(8,128)(2,1)S(1)}, bf16[1,4096,128]{2,1,0:T(8,128)(2,1)}, u32[]{:S(2)}) copy-start(bf16[1,4096,128]{2,1,0:T(8,128)(2,1)} %param.24) | copy-start | bytes 3145732
  214.6 114.8 %reduce-scatter.3.cloned.1.call-start = ((), (), s32[]{:S(2)}) async-start(), calls=%async_computation.6 | async-start | bytes 4718592 | tf_op jit(solution)/shard_map/reduce_scatter | solution.py:47
  288.5 3.0 copy-start.2
  309.7 23.5 %copy-start.7 = (bf16[16,128]{1,0:T(8,128)(2,1)S(1)}, bf16[16,128]{1,0:T(8,128)(2,1)}, u32[]{:S(2)}) copy-start(bf16[16,128]{1,0:T(8,128)(2,1)} %param.16) | copy-start | bytes 12292
  309.7 23.5 %copy-start.8 = (bf16[16,128]{1,0:T(8,128)(2,1)S(1)}, bf16[16,128]{1,0:T(8,128)(2,1)}, u32[]{:S(2)}) copy-start(bf16[16,128]{1,0:T(8,128)(2,1)} %param.15) | copy-start | bytes 12292
  309.7 101.4 %reduce-scatter.5.cloned.1.call-start = ((), (), s32[]{:S(2)}) async-start(), calls=%async_computation.7 | async-start | bytes 2228224 | tf_op jit(solution)/shard_map/reduce_scatter | solution.py:47
  412.7 15.1 %all-to-all-start.1 = ((bf16[12,8,512]{2,0,1:T(8,128)(2,1)}), bf16[12,8,512]{2,0,1:T(8,128)(2,1)S(1)}, u32[]{:S(2)}, u32[]{:S(2)}) async-start(bf16[12,8,512]{2,0,1:T(8,128)(2,1)} %copy.53), calls=%async_computation.3 | async-start | bytes 262144 | tf_op jit(solution)/shard_map/all_to_all | solution.py:164
Sparse Core Ops, SparseCore 0:
  10.2 109.7 all-gather.4
  122.1 71.8 all-gather.6
  214.7 68.1 all-gather.8
  309.8 19.6 reduce-scatter.2
  333.3 77.7 reduce-scatter.4
where the time goes:
time: 436 us; the launch traced here: 435 us
  waiting for transfers between devices  310 us (71%)
  blocking collectives  47 us (11%)
  local copies, waits for them, and re-layouts  24.3 us (6%)
  matrix products  18.8 us (4%)
  starting transfers between devices  15.1 us (3%)
  between operations  14.7 us (3%)
  other arithmetic  5.04 us (1%)
    all_gather x1, waiting for transfers between devices, in_one_piece(): lax.all_gather(both, axis, axis=dim, tiled=True)  106 us
    reduce_scatter x2, waiting for transfers between devices, own_block(): tiles = lax.psum_scatter(tiles, axes[k], scatter_dimension=0, tiled=True)  74.4 us
    all_gather x1, waiting for transfers between devices, body(): piece = lax.all_gather(slot_rows, SEQ, axis=0, tiled=True)  68.2 us
    all_gather x1, waiting for transfers between devices, body(): lax.all_gather(out_proj, SEQ, axis=0, tiled=True)  44.8 us
    all_gather x1, blocking collectives, body(): lax.all_gather(attn_local, 'rep', axis=1, tiled=True)  24.7 us
    all_gather x1, blocking collectives, in_one_piece(): lax.all_gather(both, axis, axis=dim, tiled=True)  22.3 us
  transfers between devices with their start and end apart: 7, of which 7 were waited for; matrix products, arithmetic and copies ran while one was open for 2% of the time, Pallas kernels for 0%

commit v1 on v0

--- a/solution.py
+++ b/solution.py
@@ -1,14 +1,32 @@
+import functools
 import math
 import jax
 import jax.numpy as jnp
 from jax import lax
 from jax.sharding import Mesh
 from jax.sharding import PartitionSpec as P
+from jax.lax import axis_index, axis_size, ppermute
 
 EXPERTS = 4
 CAP = 12
 SEQ = ("seq_0", "seq_1")
 GROUPS_SEQ = ("groups", "seq_0", "seq_1")
+
+
+def packet_assign(in_array, dim_at):
+    r2 = axis_size("rep")
+    state_now, fresh = (r2, axis_index("rep"))
+    piece_next, k_now = (in_array, 1)
+    while k_now < state_now:
+        tmp = ppermute(piece_next, "rep", tuple(((it, it ^ k_now) for it in range(state_now))))
+        outer = jnp.concatenate([piece_next, tmp], dim_at)
+        taken_in = jnp.concatenate([tmp, piece_next], dim_at)
+        piece_next = jnp.where(fresh & k_now == 0, outer, taken_in)
+        k_now = 2 * k_now
+    return piece_next
+
+
+convert_grid = functools.partial(packet_assign, dim_at=1)
 
 
 def in_one_piece(arrays, axis, dim, along):
@@ -116,7 +134,7 @@
         (numerator / totals[:, None]).reshape(tok_count, q_per * head_dim).astype(jnp.bfloat16)
     )
     attn_full, keys_cache, values_cache = (
-        lax.all_gather(attn_local, "rep", axis=1, tiled=True),
+        convert_grid(attn_local),
         *in_one_piece((keys_new, values_new), "rep", 1, 0),
     )
     projected = jnp.dot(

time: 436 us -> 436 us (level)
  blocking collectives: 47 us -> 22.4 us
  starting transfers between devices: 15.1 us -> 28.1 us
  waiting for transfers between devices: 310 us -> 322 us
    all_gather x1 -> x0, blocking collectives: 24.7 us -> none  [body(): lax.all_gather(attn_local, 'rep', axis=1, tiled=True)]
    ppermute x0 -> x3, starting transfers between devices: none -> 13.4 us  [packet_assign(): ppermute(piece_next, 'rep', tuple(((it, it ^ k_now) for it in range(state...]
    all_gather x1, waiting for transfers between devices: 44.8 us -> 50.7 us  [body(): lax.all_gather(out_proj, SEQ, axis=0, tiled=True)]
    ppermute x0 -> x3, waiting for transfers between devices: none -> 5.56 us  [packet_assign(): ppermute(piece_next, 'rep', tuple(((it, it ^ k_now) for it in range(state...]
  transfers between devices with their start and end apart: 7 -> 10, of which waited for: 7 -> 9; matrix products, arithmetic and copies ran while one was open for 2% -> 2% of each run, Pallas kernels for 0% -> 0%
where the time goes in v1:
time: 436 us; the launch traced here: 435 us
  waiting for transfers between devices  322 us (74%)
  starting transfers between devices  28.1 us (6%)
  local copies, waits for them, and re-layouts  24.2 us (6%)
  blocking collectives  22.4 us (5%)
  matrix products  18.8 us (4%)
  between operations  14.8 us (3%)
  other arithmetic  5.06 us (1%)
    all_gather x1, waiting for transfers between devices, in_one_piece(): lax.all_gather(both, axis, axis=dim, tiled=True)  106 us
    reduce_scatter x2, waiting for transfers between devices, own_block(): tiles = lax.psum_scatter(tiles, axes[k], scatter_dimension=0, tiled=True)  74.5 us
    all_gather x1, waiting for transfers between devices, body(): piece = lax.all_gather(slot_rows, SEQ, axis=0, tiled=True)  68.3 us
    all_gather x1, waiting for transfers between devices, body(): lax.all_gather(out_proj, SEQ, axis=0, tiled=True)  50.7 us
    all_gather x1, blocking collectives, in_one_piece(): lax.all_gather(both, axis, axis=dim, tiled=True)  22.4 us
    ppermute x3, starting transfers between devices, packet_assign(): ppermute(piece_next, 'rep', tuple(((it, it ^ k_now) for it in range(state...  13.4 us
  transfers between devices with their start and end apart: 10, of which 9 were waited for; matrix products, arithmetic and copies ran while one was open for 2% of the time, Pallas kernels for 0%

profile of v1, /device:TPU:66, one launch (start us, length us, event | category | flops | bytes accessed | tf_op | source)
XLA Modules:
  0.0 435.1 jit_solution(6313346168963385590)
XLA Ops:
  7.2 0.0 copy-start
  7.2 0.1 all-gather.5.cloned.1.call-start
  7.3 1.7 maximum_maximum_fusion
  8.9 0.1 all-gather.5.cloned.1.call-update
  9.0 0.1 all-gather.7.cloned.1.call-start
  9.1 0.7 all-gather.7.cloned.1.call-update
  9.8 0.7 reshape.156
  10.5 1.3 fusion.70
  12.5 0.9 select_reduce_fusion.1
  13.5 106.4 %all-gather.5.cloned.1.call-done = bf16[8704,256]{1,0:T(8,128)(2,1)} async-done(((bf16[272,256]{1,0:T(8,128)(2,1)}), bf16[8704,256]{1,0:T(8,128)(2,1)}) %all-gather.5.cloned.1.call-update) | async-done | bytes 4456464 | tf_op jit(solution)/shard_map/all_gather | solution.py:34
  119.9 2.8 select_reduce_fusion
  122.7 0.9 fusion.5
  123.6 0.0 copy-start.6
  123.6 0.8 fusion.22
  124.5 2.5 collective-permute-start
  127.0 3.2 collective-permute-done
  130.2 4.3 collective-permute-start.1
  134.5 2.4 collective-permute-done.1
  136.9 6.6 %collective-permute-start.2 = (bf16[16,2048]{1,0:T(8,128)(2,1)S(1)}, bf16[16,2048]{1,0:T(8,128)(2,1)S(1)}, u32[]{:S(2)}, u32[]{:S(2)}) collective-permute-start(bf16[16,2048]{1,0:T(8,128)(2,1)S(1)} %maximum_select_fusion.2), channel_id=1, source_target_pairs={{0,4},{1,5},{2,6},{3,7},{4,0},{5,1},{6,2},{7,3},{8,12},{9,13},{10,... | collective-permute-start | bytes 196616 | tf_op jit(solution)/shard_map/ppermute | solution.py:21
  143.5 0.0 copy-start.9
  143.5 0.0 copy-start.4
  143.5 0.0 copy-start.5
  143.5 50.7 %all-gather.7.cloned.1.call-done = bf16[4096,512]{1,0:T(8,128)(2,1)} async-done(((bf16[128,512]{1,0:T(8,128)(2,1)}), bf16[4096,512]{1,0:T(8,128)(2,1)}) %all-gather.7.cloned.1.call-update) | async-done | bytes 4194320 | tf_op jit(solution)/shard_map/all_gather | solution.py:142
  194.3 0.0 collective-permute-done.2
  194.3 2.8 fusion.16
  197.1 0.7 broadcast_in_dim.33
  197.8 7.0 %all-to-all-start = ((bf16[8,16,512]{2,1,0:T(8,128)(2,1)}), bf16[8,16,512]{2,1,0:T(8,128)(2,1)S(1)}, u32[]{:S(2)}, u32[]{:S(2)}) async-start(bf16[8,16,512]{2,1,0:T(8,128)(2,1)} %broadcast_in_dim.33), calls=%async_computation | async-start | bytes 262144 | tf_op jit(solution)/shard_map/all_to_all | solution.py:43
  204.8 8.0 %all-to-all-done = bf16[8,16,512]{2,1,0:T(8,128)(2,1)S(1)} async-done(((bf16[8,16,512]{2,1,0:T(8,128)(2,1)}), bf16[8,16,512]{2,1,0:T(8,128)(2,1)S(1)}, u32[]{:S(2)}, u32[]{:S(2)}) %all-to-all-start) | async-done | bytes 131104 | tf_op jit(solution)/shard_map/all_to_all | solution.py:43
  212.8 0.1 fusion.32
  213.0 0.0 copy-done.5
  213.0 0.3 select_reduce_fusion.2
  213.4 0.1 copy.48
  213.5 0.1 copy.49
  213.6 0.1 fusion.53
  213.7 0.9 fusion.1
  214.6 0.1 all-gather.9.cloned.1.call-update
  214.7 0.0 copy-start.1
  214.7 0.1 reduce-scatter.3.cloned.1.call-start
  214.8 68.3 %all-gather.9.cloned.1.call-done = bf16[32,12,4096]{2,1,0:T(8,128)(2,1)} async-done(((bf16[1,12,4096]{2,1,0:T(8,128)(2,1)}), bf16[32,12,4096]{2,1,0:T(8,128)(2,1)}) %all-gather.9.cloned.1.call-update) | async-done | bytes 3145744 | tf_op jit(solution)/shard_map/all_gather | solution.py:172
  283.0 5.6 %reshape.160 = bf16[384,4096]{1,0:T(8,128)(2,1)} reshape(bf16[32,12,4096]{2,1,0:T(8,128)(2,1)} %all-gather.9.cloned.1.call-done) | data formatting | bytes 6291456
  288.6 0.0 copy-done.1
  288.6 2.9 fusion.30
  291.6 0.0 copy-done
  291.6 0.0 copy-done.2
  291.6 7.0 %convolution_convert_fusion = bf16[384,4096]{1,0:T(8,128)(2,1)} fusion(bf16[384,4096]{1,0:T(8,128)(2,1)} %reshape.160, bf16[1,128,4096]{2,1,0:T(8,128)(2,1)S(1)} %copy-done, bf16[1,4096,128]{2,1,0:T(8,128)(2,1)S(1)} %copy-done.2, f32[384,128]{1,0:T(8,128)S(1)} %fusion.30), kind=kOutput, calls=%fused_computation.2 | convolution fusion | flops 807174144 | bytes 8585216 | tf_op jit(solution)/shard_map/dot_general | solution.py:177
  298.6 5.5 %reshape_reshape.3 = bf16[16,2,12,4096]{3,2,1,0:T(8,128)(2,1)} reshape(bf16[384,4096]{1,0:T(8,128)(2,1)} %convolution_convert_fusion) | data formatting | bytes 6291456 | tf_op jit(solution)/shard_map/reshape;reshape | solution.py:61
  304.1 5.6 %copy.51 = bf16[2,16,12,4096]{3,1,0,2:T(8,128)(2,1)} copy(bf16[2,16,12,4096]{3,2,0,1:T(8,128)(2,1)} %bitcast.61) | data formatting | bytes 6291456 | tf_op jit(solution)/shard_map/transpose | solution.py:62
  309.7 0.1 reduce-scatter.3.cloned.1.call-update
  309.7 0.0 copy-start.7
  309.7 0.0 copy-start.8
  309.7 0.1 reduce-scatter.5.cloned.1.call-start
  309.8 19.6 %reduce-scatter.3.cloned.1.call-done = bf16[16,12,4096]{2,0,1:T(8,128)(2,1)} async-done(((bf16[32,12,4096]{2,0,1:T(8,128)(2,1)}), bf16[16,12,4096]{2,0,1:T(8,128)(2,1)}) %reduce-scatter.3.cloned.1.call-update) | async-done | bytes 1572880 | tf_op jit(solution)/shard_map/reduce_scatter | solution.py:65
  329.4 3.6 copy.52
  333.1 0.1 reduce-scatter.5.cloned.1.call-update
  333.1 0.0 copy-done.7
  333.2 22.4 %all_gather.15 = bf16[32,1024]{1,0:T(8,128)(2,1)S(1)} all-gather(bf16[32,128]{1,0:T(8,128)(2,1)S(1)} %pad_maximum_fusion), channel_id=1, replica_groups=mesh['groups'=2,'seq_0'=16,'seq_1'=2,'rep'=8] {'rep'}, dimensions={1}, use_global_device_ids=true | all-gather | bytes 73728 | tf_op jit(solution)/shard_map/all_gather | solution.py:34
  355.6 0.6 fusion.79
  356.2 54.9 %reduce-scatter.5.cloned.1.call-done = bf16[1,12,4096]{2,1,0:T(8,128)(2,1)} async-done(((bf16[16,12,4096]{2,1,0:T(8,128)(2,1)}), bf16[1,12,4096]{2,1,0:T(8,128)(2,1)}) %reduce-scatter.5.cloned.1.call-update) | async-done | bytes 98320 | tf_op jit(solution)/shard_map/reduce_scatter | solution.py:65
  411.0 0.9 copy.57
  412.0 0.7 copy.53
  412.7 7.4 %all-to-all-start.1 = ((bf16[12,8,512]{2,0,1:T(8,128)(2,1)}), bf16[12,8,512]{2,0,1:T(8,128)(2,1)S(1)}, u32[]{:S(2)}, u32[]{:S(2)}) async-start(bf16[12,8,512]{2,0,1:T(8,128)(2,1)} %copy.53), calls=%async_computation.3 | async-start | bytes 262144 | tf_op jit(solution)/shard_map/all_to_all | solution.py:182
  420.1 0.2 convolution_bitcast_fusion
  420.3 7.4 %all-to-all-done.1 = bf16[12,8,512]{2,0,1:T(8,128)(2,1)S(1)} async-done(((bf16[12,8,512]{2,0,1:T(8,128)(2,1)}), bf16[12,8,512]{2,0,1:T(8,128)(2,1)S(1)}, u32[]{:S(2)}, u32[]{:S(2)}) %all-to-all-start.1) | async-done | bytes 98336 | tf_op jit(solution)/shard_map/all_to_all | solution.py:182
  427.7 0.8 fusion.15
  (29 shorter events, 0.3 us)
Async XLA Ops:
  7.2 284.4 %copy-start = (bf16[1,128,4096]{2,1,0:T(8,128)(2,1)S(1)}, bf16[1,128,4096]{2,1,0:T(8,128)(2,1)}, u32[]{:S(2)}) copy-start(bf16[1,128,4096]{2,1,0:T(8,128)(2,1)} %param.26) | copy-start | bytes 3145732
  7.2 112.7 %all-gather.5.cloned.1.call-start = ((), (), s32[]{:S(2)}) async-start(), calls=%async_computation.4 | async-start | bytes 4595712 | tf_op jit(solution)/shard_map/all_gather | solution.py:34
  9.0 185.3 %all-gather.7.cloned.1.call-start = ((), (), s32[]{:S(2)}) async-start(), calls=%async_computation.5 | async-start | bytes 4325376 | tf_op jit(solution)/shard_map/all_gather | solution.py:142
  119.9 3.7 copy-start.10
  123.6 70.7 %copy-start.6 = (bf16[16,512]{1,0:T(8,128)(2,1)S(1)}, bf16[16,512]{1,0:T(8,128)(2,1)}, u32[]{:S(2)}) copy-start(bf16[16,512]{1,0:T(8,128)(2,1)} %param.20) | copy-start | bytes 49156
  124.5 5.7 %collective-permute-start = (bf16[16,512]{1,0:T(8,128)(2,1)S(1)}, bf16[16,512]{1,0:T(8,128)(2,1)S(1)}, u32[]{:S(2)}, u32[]{:S(2)}) collective-permute-start(bf16[16,512]{1,0:T(8,128)(2,1)S(1)} %convert_element_type.81), channel_id=1, source_target_pairs={{0,1},{1,0},{2,3},{3,2},{4,5},{5,4},{6,7},{7,6},{8,9},{9,8},{10,11... | collective-permute-start | bytes 49160 | tf_op jit(solution)/shard_map/ppermute | solution.py:21
  130.2 6.7 %collective-permute-start.1 = (bf16[16,1024]{1,0:T(8,128)(2,1)S(1)}, bf16[16,1024]{1,0:T(8,128)(2,1)S(1)}, u32[]{:S(2)}, u32[]{:S(2)}) collective-permute-start(bf16[16,1024]{1,0:T(8,128)(2,1)S(1)} %maximum_select_fusion.3), channel_id=1, source_target_pairs={{0,2},{1,3},{2,0},{3,1},{4,6},{5,7},{6,4},{7,5},{8,10},{9,11},{10,... | collective-permute-start | bytes 98312 | tf_op jit(solution)/shard_map/ppermute | solution.py:21
  136.9 57.3 %collective-permute-start.2 = (bf16[16,2048]{1,0:T(8,128)(2,1)S(1)}, bf16[16,2048]{1,0:T(8,128)(2,1)S(1)}, u32[]{:S(2)}, u32[]{:S(2)}) collective-permute-start(bf16[16,2048]{1,0:T(8,128)(2,1)S(1)} %maximum_select_fusion.2), channel_id=1, source_target_pairs={{0,4},{1,5},{2,6},{3,7},{4,0},{5,1},{6,2},{7,3},{8,12},{9,13},{10,... | collective-permute-start | bytes 196616 | tf_op jit(solution)/shard_map/ppermute | solution.py:21
  143.5 61.3 %copy-start.9 = (s32[16,2]{0,1:T(2,128)S(1)}, s32[16,2]{0,1:T(2,128)}, u32[]{:S(2)}) copy-start(s32[16,2]{0,1:T(2,128)} %param.27) | copy-start | bytes 388
  143.5 69.5 %copy-start.4 = (f32[4096,4]{0,1:T(4,128)S(1)}, f32[4096,4]{0,1:T(4,128)}, u32[]{:S(2)}) copy-start(f32[4096,4]{0,1:T(4,128)} %param.23) | copy-start | bytes 196612
  143.5 69.5 %copy-start.5 = (f32[4096]{0:T(1024)S(1)}, f32[4096]{0:T(1024)}, u32[]{:S(2)}) copy-start(f32[4096]{0:T(1024)} %param.22) | copy-start | bytes 49156
  197.1 230.6 %copy-start.3 = (bf16[16,512]{1,0:T(8,128)(2,1)}, bf16[16,512]{1,0:T(8,128)(2,1)S(1)}, u32[]{:S(2)}) copy-start(bf16[16,512]{1,0:T(8,128)(2,1)S(1)} %fusion.16) | copy-start | bytes 49156
  197.8 15.0 %all-to-all-start = ((bf16[8,16,512]{2,1,0:T(8,128)(2,1)}), bf16[8,16,512]{2,1,0:T(8,128)(2,1)S(1)}, u32[]{:S(2)}, u32[]{:S(2)}) async-start(bf16[8,16,512]{2,1,0:T(8,128)(2,1)} %broadcast_in_dim.33), calls=%async_computation | async-start | bytes 262144 | tf_op jit(solution)/shard_map/all_to_all | solution.py:43
  204.8 78.2 %all-gather.9.cloned.1.call-start = ((), (), s32[]{:S(2)}) async-start(), calls=%async_computation.8 | async-start | bytes 4325376 | tf_op jit(solution)/shard_map/all_gather | solution.py:172
  214.7 74.0 %copy-start.1 = (bf16[1,4096,128]{2,1,0:T(8,128)(2,1)S(1)}, bf16[1,4096,128]{2,1,0:T(8,128)(2,1)}, u32[]{:S(2)}) copy-start(bf16[1,4096,128]{2,1,0:T(8,128)(2,1)} %param.24) | copy-start | bytes 3145732
  214.7 114.7 %reduce-scatter.3.cloned.1.call-start = ((), (), s32[]{:S(2)}) async-start(), calls=%async_computation.6 | async-start | bytes 4718592 | tf_op jit(solution)/shard_map/reduce_scatter | solution.py:65
  288.6 3.0 copy-start.2
  309.7 23.4 %copy-start.7 = (bf16[16,128]{1,0:T(8,128)(2,1)S(1)}, bf16[16,128]{1,0:T(8,128)(2,1)}, u32[]{:S(2)}) copy-start(bf16[16,128]{1,0:T(8,128)(2,1)} %param.16) | copy-start | bytes 12292
  309.7 23.4 %copy-start.8 = (bf16[16,128]{1,0:T(8,128)(2,1)S(1)}, bf16[16,128]{1,0:T(8,128)(2,1)}, u32[]{:S(2)}) copy-start(bf16[16,128]{1,0:T(8,128)(2,1)} %param.15) | copy-start | bytes 12292
  309.7 101.3 %reduce-scatter.5.cloned.1.call-start = ((), (), s32[]{:S(2)}) async-start(), calls=%async_computation.7 | async-start | bytes 2228224 | tf_op jit(solution)/shard_map/reduce_scatter | solution.py:65
  412.7 15.0 %all-to-all-start.1 = ((bf16[12,8,512]{2,0,1:T(8,128)(2,1)}), bf16[12,8,512]{2,0,1:T(8,128)(2,1)S(1)}, u32[]{:S(2)}, u32[]{:S(2)}) async-start(bf16[12,8,512]{2,0,1:T(8,128)(2,1)} %copy.53), calls=%async_computation.3 | async-start | bytes 262144 | tf_op jit(solution)/shard_map/all_to_all | solution.py:182
Sparse Core Ops, SparseCore 0:
  10.2 109.7 all-gather.4
  122.1 72.1 all-gather.6
  214.8 68.1 all-gather.8
  309.8 19.5 reduce-scatter.2
  333.3 77.7 reduce-scatter.4
